TPU v7x, 32 devices: a whole 2x2x4 slice. The times are simulated.
32 devices in a mesh: dp: 2 (over x), mp: 16 (over z, y, core).
Axes of the slice: x: 2, y: 2, z: 4, core: 2. Of those that a mesh axis runs over, the one named last changes fastest.
Arguments:
- base_rows: bfloat16 [256, 8192], P('dp', 'mp'), may hold values from -6 to 6
- layer_rows: bfloat16 [256, 8192], P('dp', 'mp'), may hold values from -6 to 6
- cross_weight: bfloat16 [8192, 8192], P(None, 'mp'), may hold values from -0.0625 to 0.0625
- cross_bias: float32 [8192], P('mp'), may hold values from -3 to 3
- upstream: bfloat16 [256, 8192], P('dp', 'mp'), may hold values from -6 to 6
Outputs:
- crossed: bfloat16 [256, 8192], P('dp', 'mp')
- grad_base: bfloat16 [256, 8192], P('dp', 'mp')
- grad_layer: bfloat16 [256, 8192], P('dp', 'mp')
- grad_weight: float32 [8192, 8192], P('dp', 'mp')
- grad_bias: float32 [8192], P('mp')
All inputs are finite; a program needn't handle non-finite values.
Results may differ from a plain program's by a relative error of at most 0.0041.
Values may be sent and summed in bfloat16 or wider, within the bound.
No kernel may reach another device: no remote copies, remote signals or barrier semaphores. Data moves between devices by JAX's collectives and lax.ppermute only.
A program may use at most 128 MiB of HBM per device.

v0:
```python
import jax
import jax.numpy as jnp
from jax import lax
from jax.sharding import PartitionSpec as P


def local(base_rows, layer_rows, cross_weight, cross_bias, upstream):
    groups = lax.axis_size("dp")
    row_block = lax.all_to_all(cross_weight, "mp", split_axis=0, concat_axis=1, tiled=True)
    full_rows = lax.all_gather(layer_rows, "mp", axis=1, tiled=True)
    mixed = jnp.dot(full_rows, cross_weight, preferred_element_type=jnp.float32) + cross_bias
    base = base_rows.astype(jnp.float32)
    crossed = (base * mixed + layer_rows.astype(jnp.float32)).astype(jnp.bfloat16)
    upper = upstream.astype(jnp.float32)
    delta = upper * base
    delta_low = delta.astype(jnp.bfloat16)
    grad_base = (upper * mixed).astype(jnp.bfloat16)
    back = lax.dot_general(
        lax.all_gather(delta_low, "mp", axis=1, tiled=True),
        row_block,
        (((1,), (1,)), ((), ())),
        preferred_element_type=jnp.float32,
    )
    grad_layer = (upper + back).astype(jnp.bfloat16)
    scale = jnp.float32(base_rows.shape[0] * groups) ** (-0.5)
    grad_weight = (
        lax.psum_scatter(
            lax.dot_general(
                full_rows, delta_low, (((0,), (0,)), ((), ())), preferred_element_type=jnp.float32
            ),
            "dp",
            scatter_dimension=0,
            tiled=True,
        )
        * scale
    )
    grad_bias = lax.psum(jnp.sum(delta, axis=0), "dp") * scale
    return (crossed, grad_base, grad_layer, grad_weight, grad_bias)


def solution(mesh):
    return jax.shard_map(
        local,
        mesh=mesh,
        in_specs=(P("dp", "mp"), P("dp", "mp"), P(None, "mp"), P("mp"), P("dp", "mp")),
        out_specs=(P("dp", "mp"), P("dp", "mp"), P("dp", "mp"), P("dp", "mp"), P("mp")),
        check_vma=False,
    )
```

profile of v0, /device:TPU:0, one launch (start us, length us, event | category | flops | bytes accessed | tf_op | source)
XLA Modules:
  0.0 428.7 jit_solution(16000133492980373238)
XLA Ops:
  7.2 0.0 all-gather.3.cloned.1.call-start
  7.2 0.7 all-gather.3.cloned.1.call-update
  7.9 0.0 all-gather.5.cloned.1.call-start
  7.9 46.0 %all-gather.3.cloned.1.call-done = bf16[128,8192]{1,0:T(8,128)(2,1)} async-done(((bf16[128,512]{1,0:T(8,128)(2,1)}), bf16[128,8192]{1,0:T(8,128)(2,1)}) %all-gather.3.cloned.1.call-update) | async-done | bytes 2097168 | tf_op jit(solution)/shard_map/all_gather | solution.py:10
  53.9 0.0 copy-start
  53.9 6.2 %fusion.3 = (bf16[128,512]{1,0:T(8,128)(2,1)}, bf16[128,512]{1,0:T(8,128)(2,1)}, bf16[128,512]{1,0:T(8,128)(2,1)}, f32[512]{0:T(512)S(1)}) fusion(bf16[128,512]{1,0:T(8,128)(2,1)} %param.9, bf16[128,512]{1,0:T(8,128)(2,1)} %param.6, bf16[128,512]{1,0:T(8,128)(2,1)} %param.5, f32[512]{0:T(512)} %param.8, bf16[128,8192]{1,0:T(8,128)(2,1)} %all-gather.3.cloned.1.call-done, ...), kind=kOutput, calls=%fused_computation.10 | convolution fusion | flops 1074527744 | bytes 11276288 | tf_op jit(solution)/shard_map/dot_general | solution.py:11
  60.1 0.0 all-gather.5.cloned.1.call-update
  60.2 0.0 reduce-scatter.2.cloned.1.call-start
  60.2 0.0 copy-done
  60.2 9.0 %convolution_bitcast_fusion = f32[8192,512]{0,1:T(8,128)} fusion(bf16[128,512]{1,0:T(8,128)(2,1)} %get-tuple-element.24, bf16[128,8192]{1,0:T(8,128)(2,1)S(1)} %copy-done), kind=kOutput, calls=%fused_computation | convolution fusion | flops 1073741824 | bytes 19005440 | tf_op jit(solution)/shard_map/dot_general | solution.py:28
  69.2 0.0 reduce-scatter.2.cloned.1.call-update
  69.2 4.8 %all-to-all-start = ((bf16[16,512,512]{2,1,0:T(8,128)(2,1)}), bf16[16,512,512]{2,1,0:T(8,128)(2,1)}, u32[]{:S(2)}, u32[]{:S(2)}) async-start(bf16[16,512,512]{2,1,0:T(8,128)(2,1)} %bitcast.12), calls=%async_computation | async-start | bytes 16777216 | tf_op jit(solution)/shard_map/all_to_all | solution.py:9
  74.0 4.9 %psum.7 = f32[512]{0:T(512)S(1)} all-reduce(f32[512]{0:T(512)S(1)} %get-tuple-element.25), channel_id=1, replica_groups=mesh['dp'=2,'mp'=16] {'dp'}, use_global_device_ids=true, to_apply=%region_2.0 | all-reduce | flops 512 | bytes 4096 | tf_op jit(solution)/shard_map/psum | solution.py:37
  79.0 0.6 broadcast_multiply_fusion.1
  79.6 154.0 %all-to-all-done = bf16[16,512,512]{2,1,0:T(8,128)(2,1)} async-done(((bf16[16,512,512]{2,1,0:T(8,128)(2,1)}), bf16[16,512,512]{2,1,0:T(8,128)(2,1)}, u32[]{:S(2)}, u32[]{:S(2)}) %all-to-all-start) | async-done | bytes 8388640 | tf_op jit(solution)/shard_map/all_to_all | solution.py:9
  233.6 0.0 copy-start.1
  233.6 12.3 %copy.12 = bf16[512,16,512]{0,2,1:T(8,128)(2,1)} copy(bf16[512,16,512]{2,0,1:T(8,128)(2,1)} %bitcast.1) | data formatting | bytes 16777216 | tf_op jit(solution)/shard_map/all_to_all | solution.py:9
  245.9 0.0 all-gather.5.cloned.1.call-done
  245.9 0.0 copy-done.1
  245.9 6.2 %fusion = bf16[128,512]{1,0:T(8,128)(2,1)} fusion(bf16[128,8192]{1,0:T(8,128)(2,1)} %all-gather.5.cloned.1.call-done, bf16[512,8192]{0,1:T(8,128)(2,1)} %bitcast.11, bf16[128,512]{1,0:T(8,128)(2,1)S(1)} %copy-done.1), kind=kOutput, calls=%fused_computation.4 | convolution fusion | flops 1073938432 | bytes 10747904 | tf_op jit(solution)/shard_map/dot_general | solution.py:18
  252.1 153.4 %reduce-scatter.2.cloned.1.call-done = f32[4096,512]{0,1:T(8,128)} async-done(((f32[8192,512]{0,1:T(8,128)}), f32[4096,512]{0,1:T(8,128)}) %reduce-scatter.2.cloned.1.call-update) | async-done | bytes 8388624 | tf_op jit(solution)/shard_map/reduce_scatter | solution.py:27
  405.5 7.8 %broadcast_multiply_fusion = f32[4096,512]{0,1:T(8,128)} fusion(f32[4096,512]{0,1:T(8,128)} %reduce-scatter.2.cloned.1.call-done), kind=kLoop, calls=%fused_computation.1 | loop fusion | flops 2097152 | bytes 16777216 | tf_op jit(solution)/shard_map/mul | solution.py:27
  413.3 8.9 %copy.13 = f32[4096,512]{1,0:T(8,128)} copy(f32[4096,512]{0,1:T(8,128)} %broadcast_multiply_fusion) | data formatting | bytes 16777216
Async XLA Ops:
  7.2 46.8 %all-gather.3.cloned.1.call-start = ((), (), s32[]{:S(2)}) async-start(), calls=%async_computation.2 | async-start | bytes 2228224 | tf_op jit(solution)/shard_map/all_gather | solution.py:10
  7.9 238.0 %all-gather.5.cloned.1.call-start = ((), (), s32[]{:S(2)}) async-start(), calls=%async_computation.3 | async-start | bytes 2228224 | tf_op jit(solution)/shard_map/all_gather | solution.py:19
  53.9 6.3 %copy-start = (bf16[128,8192]{1,0:T(8,128)(2,1)S(1)}, bf16[128,8192]{1,0:T(8,128)(2,1)}, u32[]{:S(2)}) copy-start(bf16[128,8192]{1,0:T(8,128)(2,1)} %all-gather.3.cloned.1.call-done) | copy-start | bytes 6291460
  60.2 345.3 %reduce-scatter.2.cloned.1.call-start = ((), (), s32[]{:S(2)}) async-start(), calls=%async_computation.4 | async-start | bytes 25165824 | tf_op jit(solution)/shard_map/reduce_scatter | solution.py:27
  69.2 164.3 %all-to-all-start = ((bf16[16,512,512]{2,1,0:T(8,128)(2,1)}), bf16[16,512,512]{2,1,0:T(8,128)(2,1)}, u32[]{:S(2)}, u32[]{:S(2)}) async-start(bf16[16,512,512]{2,1,0:T(8,128)(2,1)} %bitcast.12), calls=%async_computation | async-start | bytes 16777216 | tf_op jit(solution)/shard_map/all_to_all | solution.py:9
  233.6 12.3 %copy-start.1 = (bf16[128,512]{1,0:T(8,128)(2,1)S(1)}, bf16[128,512]{1,0:T(8,128)(2,1)}, u32[]{:S(2)}) copy-start(bf16[128,512]{1,0:T(8,128)(2,1)} %param.9) | copy-start | bytes 393220
Sparse Core Ops, SparseCore 0:
  10.1 43.7 all-gather.2
  60.3 143.4 all-gather.4
  206.1 199.3 reduce-scatter.1
where the time goes:
time: 429 us
  waiting for transfers between devices  354 us (83%)
  matrix products  21.4 us (5%)
  local copies, waits for them, and re-layouts  21.3 us (5%)
  between operations  13.8 us (3%)
  other arithmetic  8.35 us (2%)
  blocking collectives  4.93 us (1%)
  starting transfers between devices  4.92 us (1%)
    all_to_all x1, waiting for transfers between devices, local(): lax.all_to_all(cross_weight, 'mp', split_axis=0, concat_axis=1, tiled=True)  154 us
    reduce_scatter x1, waiting for transfers between devices, local(): lax.psum_scatter(lax.dot_general(full_rows, delta_low, (((0,), (0,)), (()...  153 us
    all_gather x1, waiting for transfers between devices, local(): full_rows = lax.all_gather(layer_rows, 'mp', axis=1, tiled=True)  46 us
    all_to_all x1, local copies, waits for them, and re-layouts, local(): lax.all_to_all(cross_weight, 'mp', split_axis=0, concat_axis=1, tiled=True)  12.3 us
    dot_general x1, matrix products, local(): lax.dot_general(full_rows, delta_low, (((0,), (0,)), ((), ())), preferred...  8.99 us
    unnamed x5, local copies, waits for them, and re-layouts  8.95 us
  transfers between devices with their start and end apart: 4, of which 3 were waited for; matrix products, arithmetic and copies ran while one was open for 7% of the time, Pallas kernels for 0%

commit v1 on v0

--- a/solution.py
+++ b/solution.py
@@ -7,7 +7,12 @@
 def local(base_rows, layer_rows, cross_weight, cross_bias, upstream):
     groups = lax.axis_size("dp")
     row_block = lax.all_to_all(cross_weight, "mp", split_axis=0, concat_axis=1, tiled=True)
-    full_rows = lax.all_gather(layer_rows, "mp", axis=1, tiled=True)
+    ring = [layer_rows]
+    for hop in range(15):
+        ring.append(lax.ppermute(ring[-1], "mp", [(dev, (dev + 1) % 16) for dev in range(16)]))
+    full_rows = jnp.roll(
+        jnp.concatenate(ring[::-1], axis=1), (lax.axis_index("mp") + 1) * ring[0].shape[1], axis=1
+    )
     mixed = jnp.dot(full_rows, cross_weight, preferred_element_type=jnp.float32) + cross_bias
     base = base_rows.astype(jnp.float32)
     crossed = (base * mixed + layer_rows.astype(jnp.float32)).astype(jnp.bfloat16)

time: 429 us -> 363 us (0.85)
  the two profiles are of different devices: /device:TPU:0 before, /device:TPU:15 now
where the time goes in v1:
time: 363 us
  waiting for transfers between devices  215 us (59%)
  starting transfers between devices  82.4 us (23%)
  matrix products  22.8 us (6%)
  between operations  15.8 us (4%)
  local copies, waits for them, and re-layouts  13.5 us (4%)
  other arithmetic  8.4 us (2%)
  blocking collectives  4.38 us (1%)
    all_to_all x1, waiting for transfers between devices, local(): lax.all_to_all(cross_weight, 'mp', split_axis=0, concat_axis=1, tiled=True)  186 us
    ppermute x15, starting transfers between devices, local(): lax.ppermute(ring[-1], 'mp', [(dev, (dev + 1) % 16) for dev in range(16)])  48.6 us
    all_to_all x1, starting transfers between devices, local(): lax.all_to_all(cross_weight, 'mp', split_axis=0, concat_axis=1, tiled=True)  33.8 us
    ppermute x15, waiting for transfers between devices, local(): lax.ppermute(ring[-1], 'mp', [(dev, (dev + 1) % 16) for dev in range(16)])  29.5 us
    all_to_all x1, local copies, waits for them, and re-layouts, local(): lax.all_to_all(cross_weight, 'mp', split_axis=0, concat_axis=1, tiled=True)  12.3 us
    dot_general x1, matrix products, local(): lax.dot_general(full_rows, delta_low, (((0,), (0,)), ((), ())), preferred...  9.71 us
    mul x1, other arithmetic, local(): lax.psum_scatter(lax.dot_general(full_rows, delta_low, (((0,), (0,)), (()...  7.82 us
  transfers between devices with their start and end apart: 18, of which 16 were waited for; matrix products, arithmetic and copies ran while one was open for 8% of the time, Pallas kernels for 0%

profile of v1, /device:TPU:15, one launch (start us, length us, event | category | flops | bytes accessed | tf_op | source)
XLA Modules:
  0.0 362.7 jit_solution(10095807290129316166)
XLA Ops:
  9.9 2.3 collective-permute-done
  12.2 3.2 collective-permute-start.1
  17.4 3.3 collective-permute-start.2
  20.7 1.9 collective-permute-done.2
  22.7 3.3 collective-permute-start.3
  26.0 1.9 collective-permute-done.3
  27.9 3.3 collective-permute-start.4
  31.3 1.9 collective-permute-done.4
  33.2 3.3 collective-permute-start.5
  36.6 1.9 collective-permute-done.5
  38.5 3.3 collective-permute-start.6
  43.8 3.3 collective-permute-start.7
  47.2 1.9 collective-permute-done.7
  49.1 3.3 collective-permute-start.8
  54.4 3.3 collective-permute-start.9
  57.8 1.9 collective-permute-done.9
  59.7 3.3 collective-permute-start.10
  63.0 1.9 collective-permute-done.10
  65.0 3.3 collective-permute-start.11
  68.3 1.9 collective-permute-done.11
  70.3 3.3 collective-permute-start.12
  73.6 1.9 collective-permute-done.12
  75.6 3.3 collective-permute-start.13
  80.9 3.3 collective-permute-start.14
  87.7 7.1 %fusion.10 = (bf16[128,512]{1,0:T(8,128)(2,1)}, bf16[128,512]{1,0:T(8,128)(2,1)}, bf16[128,512]{1,0:T(8,128)(2,1)}, f32[512]{0:T(512)S(1)}) fusion(bf16[128,512]{1,0:T(8,128)(2,1)S(1)} %copy-done.2, bf16[128,512]{1,0:T(8,128)(2,1)S(1)} %copy-done.1, bf16[128,512]{1,0:T(8,128)(2,1)S(1)} %copy-done.3, f32[512]{0:T(512)S(1)} %copy-done.4, ...), kind=kOutput, calls=%fused_computation.13 | convolution fusion | flops 1074527744 | bytes 11276292 | tf_op jit(solution)/shard_map/dot_general | solution.py:16
  94.9 9.7 %fusion = f32[8192,512]{1,0:T(8,128)} fusion(bf16[128,512]{1,0:T(8,128)(2,1)} %get-tuple-element.9, bf16[128,16384]{1,0:T(8,128)(2,1)} %copy-done, s32[]{:T(128)S(6)} %select_n.14), kind=kOutput, calls=%fused_computation.1 | convolution fusion | flops 1073741824 | bytes 19005444 | tf_op jit(solution)/shard_map/dot_general | solution.py:33
  104.7 33.8 %all-to-all-start = ((bf16[16,512,512]{2,1,0:T(8,128)(2,1)}), bf16[16,512,512]{2,1,0:T(8,128)(2,1)}, u32[]{:S(2)}, u32[]{:S(2)}) async-start(bf16[16,512,512]{2,1,0:T(8,128)(2,1)} %bitcast.7), calls=%async_computation | async-start | bytes 16777216 | tf_op jit(solution)/shard_map/all_to_all | solution.py:9
  138.4 4.4 %psum.7 = f32[512]{0:T(512)S(1)} all-reduce(f32[512]{0:T(512)S(1)} %get-tuple-element.10), channel_id=1, replica_groups=mesh['dp'=2,'mp'=16] {'dp'}, use_global_device_ids=true, to_apply=%region_2.3 | all-reduce | flops 512 | bytes 4096 | tf_op jit(solution)/shard_map/psum | solution.py:42
  143.4 185.8 %all-to-all-done = bf16[16,512,512]{2,1,0:T(8,128)(2,1)} async-done(((bf16[16,512,512]{2,1,0:T(8,128)(2,1)}), bf16[16,512,512]{2,1,0:T(8,128)(2,1)}, u32[]{:S(2)}, u32[]{:S(2)}) %all-to-all-start) | async-done | bytes 8388640 | tf_op jit(solution)/shard_map/all_to_all | solution.py:9
  329.2 12.3 %copy.10 = bf16[512,16,512]{0,2,1:T(8,128)(2,1)} copy(bf16[512,16,512]{2,0,1:T(8,128)(2,1)} %bitcast.1) | data formatting | bytes 16777216 | tf_op jit(solution)/shard_map/all_to_all | solution.py:9
  341.5 5.9 %fusion.7 = bf16[128,512]{1,0:T(8,128)(2,1)} fusion(bf16[128,8192]{1,0:T(8,128)(2,1)} %all-gather.2.cloned.1.call-done, bf16[512,8192]{0,1:T(8,128)(2,1)} %bitcast.8, bf16[128,512]{1,0:T(8,128)(2,1)S(1)} %copy-done.2), kind=kOutput, calls=%fused_computation.7 | convolution fusion | flops 1073938432 | bytes 10747904 | tf_op jit(solution)/shard_map/dot_general | solution.py:23
  347.4 7.8 %broadcast_multiply_fusion = f32[4096,512]{1,0:T(8,128)} fusion(f32[4096,512]{1,0:T(8,128)} %reduce-scatter.2.cloned.1.call-done), kind=kLoop, calls=%fused_computation | loop fusion | flops 2097152 | bytes 16777216 | tf_op jit(solution)/shard_map/mul | solution.py:32
  (55 shorter events, 13.6 us)
Async XLA Ops:
  8.0 79.6 %copy-start.1 = (bf16[128,512]{1,0:T(8,128)(2,1)S(1)}, bf16[128,512]{1,0:T(8,128)(2,1)}, u32[]{:S(2)}) copy-start(bf16[128,512]{1,0:T(8,128)(2,1)} %param.6) | copy-start | bytes 393220
  8.0 333.5 %all-gather.2.cloned.1.call-start = ((), (), s32[]{:S(2)}) async-start(), calls=%async_computation.2 | async-start | bytes 2228224 | tf_op jit(solution)/shard_map/all_gather | solution.py:24
  8.1 4.1 %collective-permute-start = (bf16[128,512]{1,0:T(8,128)(2,1)}, bf16[128,512]{1,0:T(8,128)(2,1)S(1)}, u32[]{:S(2)}, u32[]{:S(2)}) collective-permute-start(bf16[128,512]{1,0:T(8,128)(2,1)} %param.6), channel_id=1, source_target_pairs={{0,1},{1,2},{2,3},{3,4},{4,5},{5,6},{6,7},{7,8},{8,9},{9,10},{10,1... | collective-permute-start | bytes 393224 | tf_op jit(solution)/shard_map/ppermute | solution.py:12
  12.2 5.2 %collective-permute-start.1 = (bf16[128,512]{1,0:T(8,128)(2,1)S(1)}, bf16[128,512]{1,0:T(8,128)(2,1)S(1)}, u32[]{:S(2)}, u32[]{:S(2)}) collective-permute-start(bf16[128,512]{1,0:T(8,128)(2,1)S(1)} %collective-permute-done), channel_id=1, source_target_pairs={{0,1},{1,2},{2,3},{3,4},{4,5},{5,6},{6,7},{7,8},{8,9},{9,10},{10,1... | collective-permute-start | bytes 393224 | tf_op jit(solution)/shard_map/ppermute | solution.py:12
  17.4 5.3 %collective-permute-start.2 = (bf16[128,512]{1,0:T(8,128)(2,1)S(1)}, bf16[128,512]{1,0:T(8,128)(2,1)S(1)}, u32[]{:S(2)}, u32[]{:S(2)}) collective-permute-start(bf16[128,512]{1,0:T(8,128)(2,1)S(1)} %collective-permute-done.1), channel_id=1, source_target_pairs={{0,1},{1,2},{2,3},{3,4},{4,5},{5,6},{6,7},{7,8},{8,9},{9,10},{10,1... | collective-permute-start | bytes 393224 | tf_op jit(solution)/shard_map/ppermute | solution.py:12
  22.7 5.3 %collective-permute-start.3 = (bf16[128,512]{1,0:T(8,128)(2,1)S(1)}, bf16[128,512]{1,0:T(8,128)(2,1)S(1)}, u32[]{:S(2)}, u32[]{:S(2)}) collective-permute-start(bf16[128,512]{1,0:T(8,128)(2,1)S(1)} %collective-permute-done.2), channel_id=1, source_target_pairs={{0,1},{1,2},{2,3},{3,4},{4,5},{5,6},{6,7},{7,8},{8,9},{9,10},{10,1... | collective-permute-start | bytes 393224 | tf_op jit(solution)/shard_map/ppermute | solution.py:12
  27.9 5.3 %collective-permute-start.4 = (bf16[128,512]{1,0:T(8,128)(2,1)S(1)}, bf16[128,512]{1,0:T(8,128)(2,1)S(1)}, u32[]{:S(2)}, u32[]{:S(2)}) collective-permute-start(bf16[128,512]{1,0:T(8,128)(2,1)S(1)} %collective-permute-done.3), channel_id=1, source_target_pairs={{0,1},{1,2},{2,3},{3,4},{4,5},{5,6},{6,7},{7,8},{8,9},{9,10},{10,1... | collective-permute-start | bytes 393224 | tf_op jit(solution)/shard_map/ppermute | solution.py:12
  33.2 5.3 %collective-permute-start.5 = (bf16[128,512]{1,0:T(8,128)(2,1)S(1)}, bf16[128,512]{1,0:T(8,128)(2,1)S(1)}, u32[]{:S(2)}, u32[]{:S(2)}) collective-permute-start(bf16[128,512]{1,0:T(8,128)(2,1)S(1)} %collective-permute-done.4), channel_id=1, source_target_pairs={{0,1},{1,2},{2,3},{3,4},{4,5},{5,6},{6,7},{7,8},{8,9},{9,10},{10,1... | collective-permute-start | bytes 393224 | tf_op jit(solution)/shard_map/ppermute | solution.py:12
  38.5 5.3 %collective-permute-start.6 = (bf16[128,512]{1,0:T(8,128)(2,1)S(1)}, bf16[128,512]{1,0:T(8,128)(2,1)S(1)}, u32[]{:S(2)}, u32[]{:S(2)}) collective-permute-start(bf16[128,512]{1,0:T(8,128)(2,1)S(1)} %collective-permute-done.5), channel_id=1, source_target_pairs={{0,1},{1,2},{2,3},{3,4},{4,5},{5,6},{6,7},{7,8},{8,9},{9,10},{10,1... | collective-permute-start | bytes 393224 | tf_op jit(solution)/shard_map/ppermute | solution.py:12
  43.8 5.3 %collective-permute-start.7 = (bf16[128,512]{1,0:T(8,128)(2,1)S(1)}, bf16[128,512]{1,0:T(8,128)(2,1)S(1)}, u32[]{:S(2)}, u32[]{:S(2)}) collective-permute-start(bf16[128,512]{1,0:T(8,128)(2,1)S(1)} %collective-permute-done.6), channel_id=1, source_target_pairs={{0,1},{1,2},{2,3},{3,4},{4,5},{5,6},{6,7},{7,8},{8,9},{9,10},{10,1... | collective-permute-start | bytes 393224 | tf_op jit(solution)/shard_map/ppermute | solution.py:12
  49.1 5.3 %collective-permute-start.8 = (bf16[128,512]{1,0:T(8,128)(2,1)S(1)}, bf16[128,512]{1,0:T(8,128)(2,1)S(1)}, u32[]{:S(2)}, u32[]{:S(2)}) collective-permute-start(bf16[128,512]{1,0:T(8,128)(2,1)S(1)} %collective-permute-done.7), channel_id=1, source_target_pairs={{0,1},{1,2},{2,3},{3,4},{4,5},{5,6},{6,7},{7,8},{8,9},{9,10},{10,1... | collective-permute-start | bytes 393224 | tf_op jit(solution)/shard_map/ppermute | solution.py:12
  54.4 5.3 %collective-permute-start.9 = (bf16[128,512]{1,0:T(8,128)(2,1)S(1)}, bf16[128,512]{1,0:T(8,128)(2,1)S(1)}, u32[]{:S(2)}, u32[]{:S(2)}) collective-permute-start(bf16[128,512]{1,0:T(8,128)(2,1)S(1)} %collective-permute-done.8), channel_id=1, source_target_pairs={{0,1},{1,2},{2,3},{3,4},{4,5},{5,6},{6,7},{7,8},{8,9},{9,10},{10,1... | collective-permute-start | bytes 393224 | tf_op jit(solution)/shard_map/ppermute | solution.py:12
  59.7 5.3 %collective-permute-start.10 = (bf16[128,512]{1,0:T(8,128)(2,1)S(1)}, bf16[128,512]{1,0:T(8,128)(2,1)S(1)}, u32[]{:S(2)}, u32[]{:S(2)}) collective-permute-start(bf16[128,512]{1,0:T(8,128)(2,1)S(1)} %collective-permute-done.9), channel_id=1, source_target_pairs={{0,1},{1,2},{2,3},{3,4},{4,5},{5,6},{6,7},{7,8},{8,9},{9,10},{10,1... | collective-permute-start | bytes 393224 | tf_op jit(solution)/shard_map/ppermute | solution.py:12
  65.0 5.3 %collective-permute-start.11 = (bf16[128,512]{1,0:T(8,128)(2,1)S(1)}, bf16[128,512]{1,0:T(8,128)(2,1)S(1)}, u32[]{:S(2)}, u32[]{:S(2)}) collective-permute-start(bf16[128,512]{1,0:T(8,128)(2,1)S(1)} %collective-permute-done.10), channel_id=1, source_target_pairs={{0,1},{1,2},{2,3},{3,4},{4,5},{5,6},{6,7},{7,8},{8,9},{9,10},{10,1... | collective-permute-start | bytes 393224 | tf_op jit(solution)/shard_map/ppermute | solution.py:12
  70.3 5.3 %collective-permute-start.12 = (bf16[128,512]{1,0:T(8,128)(2,1)S(1)}, bf16[128,512]{1,0:T(8,128)(2,1)S(1)}, u32[]{:S(2)}, u32[]{:S(2)}) collective-permute-start(bf16[128,512]{1,0:T(8,128)(2,1)S(1)} %collective-permute-done.11), channel_id=1, source_target_pairs={{0,1},{1,2},{2,3},{3,4},{4,5},{5,6},{6,7},{7,8},{8,9},{9,10},{10,1... | collective-permute-start | bytes 393224 | tf_op jit(solution)/shard_map/ppermute | solution.py:12
  75.6 5.3 %collective-permute-start.13 = (bf16[128,512]{1,0:T(8,128)(2,1)S(1)}, bf16[128,512]{1,0:T(8,128)(2,1)S(1)}, u32[]{:S(2)}, u32[]{:S(2)}) collective-permute-start(bf16[128,512]{1,0:T(8,128)(2,1)S(1)} %collective-permute-done.12), channel_id=1, source_target_pairs={{0,1},{1,2},{2,3},{3,4},{4,5},{5,6},{6,7},{7,8},{8,9},{9,10},{10,1... | collective-permute-start | bytes 393224 | tf_op jit(solution)/shard_map/ppermute | solution.py:12
  80.9 5.3 %collective-permute-start.14 = (bf16[128,512]{1,0:T(8,128)(2,1)S(1)}, bf16[128,512]{1,0:T(8,128)(2,1)S(1)}, u32[]{:S(2)}, u32[]{:S(2)}) collective-permute-start(bf16[128,512]{1,0:T(8,128)(2,1)S(1)} %collective-permute-done.13), channel_id=1, source_target_pairs={{0,1},{1,2},{2,3},{3,4},{4,5},{5,6},{6,7},{7,8},{8,9},{9,10},{10,1... | collective-permute-start | bytes 393224 | tf_op jit(solution)/shard_map/ppermute | solution.py:12
  84.2 3.5 copy-start.2
  84.2 3.5 copy-start.3
  84.2 3.5 copy-start.4
  87.7 7.2 %copy-start = (bf16[128,16384]{1,0:T(8,128)(2,1)}, bf16[128,16384]{1,0:T(8,128)(2,1)S(1)}, u32[]{:S(2)}) copy-start(bf16[128,16384]{1,0:T(8,128)(2,1)S(1)} %constant_dynamic-update-slice_fusion) | copy-start | bytes 12582916
  94.9 252.6 %reduce-scatter.2.cloned.1.call-start = ((), (), s32[]{:S(2)}) async-start(), calls=%async_computation.3 | async-start | bytes 25165824 | tf_op jit(solution)/shard_map/reduce_scatter | solution.py:32
  104.7 224.6 %all-to-all-start = ((bf16[16,512,512]{2,1,0:T(8,128)(2,1)}), bf16[16,512,512]{2,1,0:T(8,128)(2,1)}, u32[]{:S(2)}, u32[]{:S(2)}) async-start(bf16[16,512,512]{2,1,0:T(8,128)(2,1)} %bitcast.7), calls=%async_computation | async-start | bytes 16777216 | tf_op jit(solution)/shard_map/all_to_all | solution.py:9
Sparse Core Ops, SparseCore 0:
  95.0 116.8 all-gather.1
Sparse Core Ops, SparseCore 1:
  104.8 213.7 reduce-scatter.1
